TPU v7x, 32 devices: a whole 2x2x4 slice. The times are simulated.
32 devices in a mesh: prow: 8 (over z, core), pcol: 4 (over y, x).
Axes of the slice: x: 2, y: 2, z: 4, core: 2. Of those that a mesh axis runs over, the one named last changes fastest.
Arguments:
- matrix: float32 [8192, 24576], P('prow', 'pcol'), may hold values from -14 to 104.50967, as said below
Outputs:
- factored: float32 [8192, 24576], P('prow', 'pcol')
- tfactors: float32 [2, 128, 128], replicated
Inputs may be any that keep to these rules, and one draw needn't show every extreme that they name: `matrix`: real entries.
All inputs are finite; a program needn't handle non-finite values.
Results may differ from a plain program's by a relative error of at most 0.0003.
Values sent between devices are 32-bit elements; how exact they have to be, the bound alone decides.
A program may use at most 192 MiB of HBM per device.

v0:
```python
import jax
import jax.numpy as jnp
from jax import lax
from jax.sharding import PartitionSpec as P

NB = 128
highest = lax.Precision.HIGHEST


def broadcast(value, axis, root):
    mine = lax.axis_index(axis) == root
    return lax.psum(jnp.where(mine, value, jnp.zeros_like(value)), axis)


def transposed_product(left, right):
    return lax.dot_general(
        left, right, (((0,), (0,)), ((), ())), precision=highest, preferred_element_type=jnp.float32
    )


def matmul(left, right):
    return jnp.dot(left, right, precision=highest, preferred_element_type=jnp.float32)


def unit_inverse(strict_part):
    size_now = strict_part.shape[0]
    identity = jnp.eye(size_now, dtype=jnp.float32)
    term = identity
    total = identity
    for power in range(size_now - 1):
        term = -matmul(term, strict_part)
        total = total + term
    return total


def cholesky_pair(square):
    block_size = square.shape[0]
    if block_size <= 8:
        row_ids = jnp.arange(block_size)
        lower_part = jnp.zeros((block_size, block_size), jnp.float32)
        working = square
        for column in range(block_size):
            pivot = jnp.sqrt(working[column, column])
            column_values = jnp.where(row_ids >= column, working[:, column] / pivot, 0.0)
            lower_part = (
                lower_part
                + column_values[:, None] * (row_ids == column).astype(jnp.float32)[None, :]
            )
            working = working - column_values[:, None] * column_values[None, :]
        diagonal_values = jnp.diagonal(lower_part)
        unit_part = lower_part / diagonal_values[None, :]
        identity = jnp.eye(block_size, dtype=jnp.float32)
        lower_inverse = unit_inverse(unit_part - identity) / diagonal_values[:, None]
        return (lower_part, lower_inverse)
    middle = block_size // 2
    top_lower, top_inverse = cholesky_pair(square[:middle, :middle])
    left_lower = matmul(square[middle:, :middle], top_inverse.T)
    rest_lower, rest_inverse = cholesky_pair(
        square[middle:, middle:] - matmul(left_lower, left_lower.T)
    )
    zero_block = jnp.zeros((middle, block_size - middle), jnp.float32)
    lower_part = jnp.block([[top_lower, zero_block], [left_lower, rest_lower]])
    corner_inverse = -matmul(rest_inverse, matmul(left_lower, top_inverse))
    lower_inverse = jnp.block([[top_inverse, zero_block], [corner_inverse, rest_inverse]])
    return (lower_part, lower_inverse)


def lower_upper(square):
    block_size = square.shape[0]
    identity = jnp.eye(block_size, dtype=jnp.float32)
    if block_size <= 8:
        row_ids = jnp.arange(block_size)
        lower_part = identity
        working = square
        for column in range(block_size):
            multipliers = jnp.where(
                row_ids > column, working[:, column] / working[column, column], 0.0
            )
            lower_part = (
                lower_part + multipliers[:, None] * (row_ids == column).astype(jnp.float32)[None, :]
            )
            working = working - multipliers[:, None] * working[column, :][None, :]
        upper_part = jnp.triu(working)
        lower_inverse = unit_inverse(lower_part - identity)
        diagonal_values = jnp.diagonal(upper_part)
        upper_inverse = (
            unit_inverse(upper_part / diagonal_values[:, None] - identity)
            / diagonal_values[None, :]
        )
        return (lower_part, lower_inverse, upper_part, upper_inverse)
    middle = block_size // 2
    top_lower, top_lower_inv, top_upper, top_upper_inv = lower_upper(square[:middle, :middle])
    right_upper = matmul(top_lower_inv, square[:middle, middle:])
    left_lower = matmul(square[middle:, :middle], top_upper_inv)
    rest_lower, rest_lower_inv, rest_upper, rest_upper_inv = lower_upper(
        square[middle:, middle:] - matmul(left_lower, right_upper)
    )
    zero_block = jnp.zeros((middle, block_size - middle), jnp.float32)
    lower_part = jnp.block([[top_lower, zero_block], [left_lower, rest_lower]])
    upper_part = jnp.block([[top_upper, right_upper], [zero_block.T, rest_upper]])
    lower_corner = -matmul(rest_lower_inv, matmul(left_lower, top_lower_inv))
    upper_corner = -matmul(top_upper_inv, matmul(right_upper, rest_upper_inv))
    lower_inverse = jnp.block([[top_lower_inv, zero_block], [lower_corner, rest_lower_inv]])
    upper_inverse = jnp.block([[top_upper_inv, upper_corner], [zero_block.T, rest_upper_inv]])
    return (lower_part, lower_inverse, upper_part, upper_inverse)


def factor_panel(panel_cols, first_row, global_rows, my_row):
    rows_dev = panel_cols.shape[0]
    offset = first_row % rows_dev
    is_owner = my_row == first_row // rows_dev
    masked = jnp.where((global_rows >= first_row)[:, None], panel_cols, 0.0)
    corner = jnp.where(is_owner, panel_cols[offset : offset + NB], 0.0)
    gram_matrix, top_block = lax.psum((transposed_product(masked, masked), corner), "prow")
    identity = jnp.eye(NB, dtype=jnp.float32)
    chol_lower, chol_inverse = cholesky_pair(gram_matrix)
    upper_inverse = chol_inverse.T
    square = identity + matmul(top_block, upper_inverse)
    unit_lower, lower_inverse, wy_upper, wy_inverse = lower_upper(square)
    reflectors = matmul(masked, matmul(upper_inverse, wy_inverse))
    patched = reflectors.at[offset : offset + NB].add(wy_inverse)
    reflectors = jnp.where(is_owner, patched, reflectors)
    tfactor = matmul(wy_upper, lower_inverse.T)
    corner_packed = jnp.triu(-chol_lower.T) + jnp.tril(unit_lower, -1)
    packed_panel = jnp.where((global_rows < first_row)[:, None], panel_cols, reflectors)
    packed_panel = jnp.where(
        is_owner, packed_panel.at[offset : offset + NB].set(corner_packed), packed_panel
    )
    return (reflectors, tfactor, packed_panel)


def per_device(matrix):
    rows_dev, cols_dev = matrix.shape
    my_row = lax.axis_index("prow")
    my_col = lax.axis_index("pcol")
    global_rows = my_row * rows_dev + jnp.arange(rows_dev, dtype=jnp.int32)
    own_cols = my_col * cols_dev + jnp.arange(cols_dev, dtype=jnp.int32)
    owned = matrix
    panels = broadcast(matrix[:, : 2 * NB], "pcol", 0)
    factors = []
    packed_results = []
    for panel_index in range(2):
        first_row = panel_index * NB
        source = panels[:, first_row : first_row + NB]
        reflectors, tfactor, packed_panel = factor_panel(source, first_row, global_rows, my_row)
        if panel_index == 0:
            target = jnp.concatenate([panels[:, NB : 2 * NB], owned], axis=1)
            target_ids = jnp.concatenate([NB + jnp.arange(NB, dtype=jnp.int32), own_cols])
        else:
            target = owned
            target_ids = own_cols
        products = lax.psum(transposed_product(reflectors, target), "prow")
        update = matmul(reflectors, matmul(tfactor.T, products))
        target = jnp.where((target_ids >= first_row + NB)[None, :], target - update, target)
        if panel_index == 0:
            panels = jnp.concatenate([panels[:, :NB], target[:, :NB]], axis=1)
            owned = target[:, NB:]
        else:
            owned = target
        factors.append(tfactor)
        packed_results.append(packed_panel)
    first_t, second_t = factors
    leading_packed_panel, following_packed_panel = packed_results
    packed_both = jnp.concatenate([leading_packed_panel, following_packed_panel], axis=1)
    result = owned.at[:, : 2 * NB].set(jnp.where(my_col == 0, packed_both, owned[:, : 2 * NB]))
    return (result, jnp.stack([first_t, second_t]))


def solution(mesh):
    placed = (P("prow", "pcol"),)
    return jax.shard_map(
        per_device, mesh=mesh, in_specs=placed, out_specs=(P("prow", "pcol"), P()), check_vma=False
    )
```

profile of v0, /device:TPU:0, one launch (start us, length us, event | category | flops | bytes accessed | tf_op | source)
XLA Modules:
  0.0 1456.2 jit_solution(11789288657180956184)
XLA Ops:
  7.2 1.3 slice.4711
  8.9 1.0 broadcast_select_fusion
  11.3 0.7 copy.2036
  12.1 0.7 compare_reduce_fusion
  14.2 52.6 %all-reduce.188.cloned.1.call-done = f32[1024,256]{0,1:T(8,128)} async-done(((f32[1024,256]{0,1:T(8,128)}), f32[1024,256]{0,1:T(8,128)}) %all-reduce.188.cloned.1.call-update) | async-done | bytes 1048592 | tf_op jit(solution)/shard_map/psum | solution.py:12
  66.8 1.6 slice_select_fusion.5
  68.4 2.4 fusion.169
  71.5 54.6 %all-reduce.196.cloned.1.call-done = (f32[128,128]{1,0:T(8,128)}, f32[128,128]{0,1:T(8,128)}) async-done(((f32[128,128]{1,0:T(8,128)}, f32[128,128]{0,1:T(8,128)}), (f32[128,128]{1,0:T(8,128)}, f32[128,128]{0,1:T(8,128)})) %all-reduce.196.cloned.1.call-update) | async-done | bytes 131088 | tf_op jit(solution)/shard_map/psum | solution.py:114
  126.1 1.2 slice.6316
  128.0 0.8 fusion.1096
  128.8 0.7 slice_subtract_fusion.31
  131.0 0.7 multiply_subtract_fusion.415
  133.2 0.8 multiply_subtract_fusion.414
  135.4 0.8 multiply_subtract_fusion.413
  137.7 0.8 multiply_subtract_fusion.412
  139.9 0.8 multiply_subtract_fusion.411
  142.1 0.8 multiply_subtract_fusion.410
  146.0 0.8 fusion.1089
  147.0 0.8 convolution_subtract_fusion.59
  161.9 0.8 fusion.593
  162.9 0.8 convolution_subtract_fusion.27
  192.4 0.9 fusion.470
  193.4 0.9 convolution_subtract_fusion.11
  252.0 1.0 fusion.351
  253.2 0.9 convolution_subtract_fusion.3
  370.2 1.1 convolution_add_fusion.1
  429.2 0.7 fusion.1307
  556.8 0.7 fusion.1315
  626.5 0.8 slice_select_fusion
  627.5 19.9 %fusion.2 = f32[128,6272]{1,0:T(8,128)} fusion(f32[1024,128]{0,1:T(8,128)S(1)} %fusion.181, f32[1024,6144]{1,0:T(8,128)} %param.11, f32[1024,128]{1,0:T(8,128)S(1)} %copy.1064), kind=kOutput, calls=%fused_computation.69 | convolution fusion | flops 9871425536 | bytes 29425664 | tf_op jit(solution)/shard_map/dot_general | solution.py:16
  652.3 72.5 %all-reduce.190.cloned.1.call-done = f32[128,6272]{1,0:T(8,128)} async-done(((f32[128,6272]{1,0:T(8,128)}), f32[128,6272]{1,0:T(8,128)}) %all-reduce.190.cloned.1.call-update) | async-done | bytes 3211280 | tf_op jit(solution)/shard_map/psum | solution.py:152
  724.7 4.9 fusion.1888
  729.7 26.5 %subtract_select_fusion = f32[1024,6272]{1,0:T(8,128)} fusion(f32[1024,6144]{1,0:T(8,128)} %param.11, f32[1024,128]{1,0:T(8,128)S(1)} %copy.1064, f32[1024,128]{0,1:T(8,128)S(1)} %fusion.181, f32[128,6272]{1,0:T(8,128)S(1)} %fusion.1888, pred[6272]{0:T(1024)(128)(4,1)S(1)} %add_compare_fusion), kind=kOutput, calls=%fused_computation.64 | convolution fusion | flops 9884270592 | bytes 55122048 | tf_op jit(solution)/shard_map/dot_general | solution.py:22
  756.2 1.1 slice.6449
  757.2 1.5 slice_select_fusion.4
  758.9 1.2 fusion.166
  760.8 54.7 %all-reduce.194.cloned.1.call-done = (f32[128,128]{1,0:T(8,128)}, f32[128,128]{1,0:T(8,128)}) async-done(((f32[128,128]{1,0:T(8,128)}, f32[128,128]{1,0:T(8,128)}), (f32[128,128]{1,0:T(8,128)}, f32[128,128]{1,0:T(8,128)})) %all-reduce.194.cloned.1.call-update) | async-done | bytes 131088 | tf_op jit(solution)/shard_map/psum | solution.py:114
  815.5 1.2 slice.6451
  817.4 0.8 fusion.1104
  818.2 0.7 slice_subtract_fusion.15
  820.4 0.7 multiply_subtract_fusion.207
  822.6 0.8 multiply_subtract_fusion.206
  824.8 0.8 multiply_subtract_fusion.205
  827.1 0.8 multiply_subtract_fusion.204
  829.3 0.8 multiply_subtract_fusion.203
  831.5 0.8 multiply_subtract_fusion.202
  835.4 0.8 fusion.1041
  836.3 0.8 convolution_subtract_fusion.43
  851.4 0.8 fusion.569
  852.2 0.8 convolution_subtract_fusion.19
  881.9 0.9 fusion.455
  882.8 0.9 convolution_subtract_fusion.7
  941.6 1.0 fusion.337
  942.6 0.9 convolution_subtract_fusion.1
  994.6 1.0 slice.5664
  1060.2 1.1 convolution_add_fusion
  1310.5 0.8 select_reduce_fusion
  1320.7 18.9 %fusion = f32[128,6144]{1,0:T(8,128)} fusion(f32[1024,128]{1,0:T(8,128)S(1)} %constant_dynamic-update-slice_fusion, f32[1024,6272]{1,0:T(8,128)} %subtract_select_fusion), kind=kOutput, calls=%fused_computation.67 | convolution fusion | flops 9663676416 | bytes 28835840 | tf_op jit(solution)/shard_map/dot_general | solution.py:16
  1343.2 0.7 pad_maximum_fusion.2
  1343.8 1.3 broadcast_select_fusion.1
  1345.3 70.3 %all-reduce.192.cloned.1.call-done = f32[128,6144]{1,0:T(8,128)} async-done(((f32[128,6144]{1,0:T(8,128)}), f32[128,6144]{1,0:T(8,128)}) %all-reduce.192.cloned.1.call-update) | async-done | bytes 3145744 | tf_op jit(solution)/shard_map/psum | solution.py:152
  1415.6 4.7 fusion.1934
  1420.3 25.9 %subtract_select_fusion.1 = f32[1024,6144]{1,0:T(8,128)} fusion(f32[1024,6272]{1,0:T(8,128)} %subtract_select_fusion, pred[6144]{0:T(1024)(128)(4,1)S(1)} %broadcast_compare_fusion, f32[1024,128]{1,0:T(8,128)S(1)} %constant_dynamic-update-slice_fusion, f32[128,6144]{1,0:T(8,128)S(1)} %fusion.1934), kind=kOutput, calls=%fused_computation.65 | convolution fusion | flops 9676259328 | bytes 54007808 | tf_op jit(solution)/shard_map/dot_general | solution.py:22
  1446.2 3.0 fusion.163
  (3322 shorter events, 801.7 us)
Async XLA Ops:
  7.2 59.6 %all-reduce.188.cloned.1.call-start = ((), (), s32[]{:S(2)}) async-start(), calls=%async_computation | async-start | bytes 2097152 | tf_op jit(solution)/shard_map/psum | solution.py:12
  9.9 116.2 %all-reduce.196.cloned.1.call-start = ((), (), s32[]{:S(2)}) async-start(), calls=%async_computation.4 | async-start | bytes 262144 | tf_op jit(solution)/shard_map/psum | solution.py:114
  10.0 0.6 copy-start.3
  66.8 558.9 %copy-start = (f32[1024,256]{0,1:T(8,128)S(1)}, f32[1024,256]{0,1:T(8,128)}, u32[]{:S(2)}) copy-start(f32[1024,256]{0,1:T(8,128)} %all-reduce.188.cloned.1.call-done) | copy-start | bytes 3145732
  70.8 653.9 %all-reduce.190.cloned.1.call-start = ((), (), s32[]{:S(2)}) async-start(), calls=%async_computation.1 | async-start | bytes 6422528 | tf_op jit(solution)/shard_map/psum | solution.py:152
  647.4 168.0 %all-reduce.194.cloned.1.call-start = ((), (), s32[]{:S(2)}) async-start(), calls=%async_computation.3 | async-start | bytes 262144 | tf_op jit(solution)/shard_map/psum | solution.py:114
  729.6 29.3 %copy-start.2 = (pred[1024]{0:T(1024)(128)(4,1)S(1)}, pred[1024]{0:T(1024)(128)(4,1)}, u32[]{:S(2)}) copy-start(pred[1024]{0:T(1024)(128)(4,1)} %fusion.1094) | copy-start | bytes 3076
  729.7 30.8 %copy-start.4 = (s32[128]{0:T(128)S(1)}, s32[128]{0:T(128)}, u32[]{:S(2)}) copy-start(s32[128]{0:T(128)} %copy-done.3) | copy-start | bytes 1540
  756.2 427.5 %copy-start.1 = (pred[8,8]{1,0:T(8,128)(4,1)S(1)}, pred[8,8]{1,0:T(8,128)(4,1)}, u32[]{:S(2)}) copy-start(pred[8,8]{1,0:T(8,128)(4,1)} %copy.1866) | copy-start | bytes 196
  756.2 554.3 %copy-start.5 = (pred[8,1]{1,0:T(8,128)(4,1)S(1)}, pred[8,1]{1,0:T(8,128)(4,1)}, u32[]{:S(2)}) copy-start(pred[8,1]{1,0:T(8,128)(4,1)} %copy.2036) | copy-start | bytes 28
  760.2 655.4 %all-reduce.192.cloned.1.call-start = ((), (), s32[]{:S(2)}) async-start(), calls=%async_computation.2 | async-start | bytes 6291456 | tf_op jit(solution)/shard_map/psum | solution.py:152
  1185.4 158.5 %copy-start.6 = (pred[1024]{0:T(1024)(128)(4,1)S(1)}, pred[1024]{0:T(1024)(128)(4,1)}, u32[]{:S(2)}) copy-start(pred[1024]{0:T(1024)(128)(4,1)} %fusion.1092) | copy-start | bytes 3076
Sparse Core Ops, SparseCore 0:
  11.6 55.1 all-reduce.187
  70.9 55.1 all-reduce.195
  647.6 77.1 all-reduce.189
  760.3 55.1 all-reduce.193
  1339.7 75.8 all-reduce.191
where the time goes:
time: 1470 us; the launch traced here: 1460 us
  local copies, waits for them, and re-layouts  395 us (27%)
  waiting for transfers between devices  305 us (21%)
  other arithmetic  287 us (20%)
  matrix products  270 us (18%)
  between operations  198 us (13%)
    dot_general x1014, matrix products, matmul(): jnp.dot(left, right, precision=highest, preferred_element_type=jnp.float32)  228 us
    mul x255, other arithmetic, lower_upper(): working = working - multipliers[:, None] * working[column, :][None, :]  166 us
    slice x256, local copies, waits for them, and re-layouts, cholesky_pair(): pivot = jnp.sqrt(working[column, column])  150 us
    slice x256, local copies, waits for them, and re-layouts, lower_upper(): working[column, column]  148 us
    psum x2, waiting for transfers between devices, per_device(): products = lax.psum(transposed_product(reflectors, target), 'prow')  143 us
    psum x2, waiting for transfers between devices, factor_panel(): lax.psum((transposed_product(masked, masked), corner), 'prow')  109 us
    psum x1, waiting for transfers between devices, broadcast(): return lax.psum(jnp.where(mine, value, jnp.zeros_like(value)), axis)  52.6 us
    slice x255, local copies, waits for them, and re-layouts, lower_upper(): working = working - multipliers[:, None] * working[column, :][None, :]  44.5 us
  transfers between devices with their start and end apart: 5, of which 5 were waited for; matrix products, arithmetic and copies ran while one was open for 1% of the time, Pallas kernels for 0%

commit v1 on v0

--- a/solution.py
+++ b/solution.py
@@ -149,7 +149,7 @@
         else:
             target = owned
             target_ids = own_cols
-        products = lax.psum(transposed_product(reflectors, target), "prow")
+        products = jnp.sum(lax.all_gather(transposed_product(reflectors, target), "prow"), axis=0)
         update = matmul(reflectors, matmul(tfactor.T, products))
         target = jnp.where((target_ids >= first_row + NB)[None, :], target - update, target)
         if panel_index == 0:

time: 1470 us -> 1780 us (1.21)
  waiting for transfers between devices: 305 us -> 585 us
  other arithmetic: 287 us -> 319 us
    all_gather x0 -> x2, waiting for transfers between devices: none -> 420 us  [per_device(): lax.all_gather(transposed_product(reflectors, target), 'prow')]
    psum x2 -> x0, waiting for transfers between devices: 143 us -> none  [per_device(): products = lax.psum(transposed_product(reflectors, target), 'prow')]
    reduce_sum x0 -> x2, other arithmetic: none -> 19.3 us  [per_device(): jnp.sum(lax.all_gather(transposed_product(reflectors, target), 'prow'), a...]
where the time goes in v1:
time: 1780 us; the launch traced here: 1760 us
  waiting for transfers between devices  585 us (33%)
  local copies, waits for them, and re-layouts  394 us (22%)
  other arithmetic  319 us (18%)
  matrix products  268 us (15%)
  between operations  199 us (11%)
    all_gather x2, waiting for transfers between devices, per_device(): lax.all_gather(transposed_product(reflectors, target), 'prow')  420 us
    dot_general x1014, matrix products, matmul(): jnp.dot(left, right, precision=highest, preferred_element_type=jnp.float32)  225 us
    mul x255, other arithmetic, lower_upper(): working = working - multipliers[:, None] * working[column, :][None, :]  166 us
    slice x256, local copies, waits for them, and re-layouts, cholesky_pair(): pivot = jnp.sqrt(working[column, column])  149 us
    slice x256, local copies, waits for them, and re-layouts, lower_upper(): working[column, column]  148 us
    psum x2, waiting for transfers between devices, factor_panel(): lax.psum((transposed_product(masked, masked), corner), 'prow')  108 us
    psum x1, waiting for transfers between devices, broadcast(): return lax.psum(jnp.where(mine, value, jnp.zeros_like(value)), axis)  56.6 us
    slice x255, local copies, waits for them, and re-layouts, lower_upper(): working = working - multipliers[:, None] * working[column, :][None, :]  44.3 us
  transfers between devices with their start and end apart: 5, of which 5 were waited for; matrix products, arithmetic and copies ran while one was open for 1% of the time, Pallas kernels for 0%

profile of v1, /device:TPU:0, one launch (start us, length us, event | category | flops | bytes accessed | tf_op | source)
XLA Modules:
  0.0 1764.3 jit_solution(13479496108566737562)
XLA Ops:
  7.2 1.3 slice.4711
  8.9 1.0 broadcast_select_fusion
  10.2 56.6 %all-reduce.186.cloned.1.call-done = f32[1024,256]{0,1:T(8,128)} async-done(((f32[1024,256]{0,1:T(8,128)}), f32[1024,256]{0,1:T(8,128)}) %all-reduce.186.cloned.1.call-update) | async-done | bytes 1048592 | tf_op jit(solution)/shard_map/psum | solution.py:12
  66.8 1.6 slice_select_fusion.5
  68.4 2.4 fusion.169
  70.9 55.2 %all-reduce.190.cloned.1.call-done = (f32[128,128]{1,0:T(8,128)}, f32[128,128]{0,1:T(8,128)}) async-done(((f32[128,128]{1,0:T(8,128)}, f32[128,128]{0,1:T(8,128)}), (f32[128,128]{1,0:T(8,128)}, f32[128,128]{0,1:T(8,128)})) %all-reduce.190.cloned.1.call-update) | async-done | bytes 131088 | tf_op jit(solution)/shard_map/psum | solution.py:114
  126.1 1.2 slice.6316
  128.0 0.8 fusion.1096
  128.8 0.7 slice_subtract_fusion.31
  131.0 0.7 multiply_subtract_fusion.415
  133.2 0.8 multiply_subtract_fusion.414
  135.4 0.8 multiply_subtract_fusion.413
  137.7 0.8 multiply_subtract_fusion.412
  139.9 0.8 multiply_subtract_fusion.411
  142.1 0.8 multiply_subtract_fusion.410
  146.0 0.8 fusion.1089
  146.8 0.8 convolution_subtract_fusion.59
  161.9 0.8 fusion.593
  162.8 0.8 convolution_subtract_fusion.27
  192.4 0.9 fusion.470
  193.3 0.9 convolution_subtract_fusion.11
  252.0 1.0 fusion.351
  253.0 0.9 convolution_subtract_fusion.3
  370.2 1.1 convolution_add_fusion.1
  383.8 0.7 fusion.1842
  628.6 1.0 gather_fusion.31
  634.2 1.0 slice_select_fusion
  635.4 20.0 %fusion.2 = f32[128,6272]{1,0:T(8,128)} fusion(f32[1024,128]{0,1:T(8,128)S(1)} %fusion.181, f32[1024,6144]{1,0:T(8,128)} %param.11, f32[1024,128]{1,0:T(8,128)S(1)} %copy.1064), kind=kOutput, calls=%fused_computation.69 | convolution fusion | flops 9871425536 | bytes 29425664 | tf_op jit(solution)/shard_map/dot_general | solution.py:16
  661.8 217.2 %all-gather.5.cloned.1.call-done = f32[1024,6272]{1,0:T(8,128)} async-done(((f32[128,6272]{1,0:T(8,128)}), f32[1024,6272]{1,0:T(8,128)}) %all-gather.5.cloned.1.call-update) | async-done | bytes 25690128 | tf_op jit(solution)/shard_map/all_gather | solution.py:152
  878.9 9.9 reduce_sum.18
  888.8 2.9 fusion.1888
  891.7 27.1 %subtract_select_fusion = f32[1024,6272]{1,0:T(8,128)} fusion(f32[1024,6144]{1,0:T(8,128)} %param.11, f32[1024,128]{1,0:T(8,128)} %copy-done.2, f32[1024,128]{0,1:T(8,128)} %copy-done, f32[128,6272]{1,0:T(8,128)S(1)} %fusion.1888, pred[6272]{0:T(1024)(128)(4,1)} %add_compare_fusion), kind=kOutput, calls=%fused_computation.64 | convolution fusion | flops 9884270592 | bytes 55122048 | tf_op jit(solution)/shard_map/dot_general | solution.py:22
  918.8 1.5 slice_select_fusion.4
  920.3 1.1 slice.6449
  921.6 1.2 fusion.166
  923.3 53.0 %all-reduce.188.cloned.1.call-done = (f32[128,128]{1,0:T(8,128)}, f32[128,128]{1,0:T(8,128)}) async-done(((f32[128,128]{1,0:T(8,128)}, f32[128,128]{1,0:T(8,128)}), (f32[128,128]{1,0:T(8,128)}, f32[128,128]{1,0:T(8,128)})) %all-reduce.188.cloned.1.call-update) | async-done | bytes 131088 | tf_op jit(solution)/shard_map/psum | solution.py:114
  976.3 1.2 slice.6451
  978.2 0.8 fusion.1104
  979.0 0.7 slice_subtract_fusion.15
  981.2 0.7 multiply_subtract_fusion.207
  983.4 0.8 multiply_subtract_fusion.206
  985.6 0.8 multiply_subtract_fusion.205
  987.9 0.8 multiply_subtract_fusion.204
  990.1 0.8 multiply_subtract_fusion.203
  992.3 0.8 multiply_subtract_fusion.202
  996.2 0.8 fusion.1041
  997.1 0.8 convolution_subtract_fusion.43
  1012.1 0.8 fusion.569
  1013.0 0.8 convolution_subtract_fusion.19
  1042.6 0.9 fusion.455
  1043.5 0.9 convolution_subtract_fusion.7
  1102.2 1.0 fusion.337
  1103.2 0.9 convolution_subtract_fusion.1
  1220.7 1.1 convolution_add_fusion
  1470.4 0.8 select_reduce_fusion
  1477.4 19.0 %fusion = f32[128,6144]{1,0:T(8,128)} fusion(f32[1024,128]{1,0:T(8,128)S(1)} %constant_dynamic-update-slice_fusion, f32[1024,6272]{1,0:T(8,128)} %subtract_select_fusion), kind=kOutput, calls=%fused_computation.67 | convolution fusion | flops 9663676416 | bytes 28835840 | tf_op jit(solution)/shard_map/dot_general | solution.py:16
  1499.7 1.0 copy.2121
  1509.3 2.1 broadcast_select_fusion.1
  1511.4 1.6 fusion.193
  1513.0 202.5 %all-gather.7.cloned.1.call-done = f32[1024,6144]{1,0:T(8,128)} async-done(((f32[128,6144]{1,0:T(8,128)}), f32[1024,6144]{1,0:T(8,128)}) %all-gather.7.cloned.1.call-update) | async-done | bytes 25165840 | tf_op jit(solution)/shard_map/all_gather | solution.py:152
  1715.5 9.4 reduce_sum.19
  1725.0 3.0 fusion.1934
  1728.0 26.3 %subtract_select_fusion.1 = f32[1024,6144]{1,0:T(8,128)} fusion(f32[1024,6272]{1,0:T(8,128)} %subtract_select_fusion, pred[6144]{0:T(1024)(128)(4,1)S(1)} %broadcast_compare_fusion, f32[1024,128]{1,0:T(8,128)} %copy-done.1, f32[128,6144]{1,0:T(8,128)S(1)} %fusion.1934), kind=kOutput, calls=%fused_computation.65 | convolution fusion | flops 9676259328 | bytes 54007808 | tf_op jit(solution)/shard_map/dot_general | solution.py:22
  1754.3 3.0 fusion.163
  (3434 shorter events, 811.9 us)
Async XLA Ops:
  7.2 59.6 %all-reduce.186.cloned.1.call-start = ((), (), s32[]{:S(2)}) async-start(), calls=%async_computation | async-start | bytes 2097152 | tf_op jit(solution)/shard_map/psum | solution.py:12
  9.9 116.2 %all-reduce.190.cloned.1.call-start = ((), (), s32[]{:S(2)}) async-start(), calls=%async_computation.4 | async-start | bytes 262144 | tf_op jit(solution)/shard_map/psum | solution.py:114
  66.8 566.7 %copy-start.3 = (f32[1024,256]{0,1:T(8,128)S(1)}, f32[1024,256]{0,1:T(8,128)}, u32[]{:S(2)}) copy-start(f32[1024,256]{0,1:T(8,128)} %all-reduce.186.cloned.1.call-done) | copy-start | bytes 3145732
  70.8 808.1 %all-gather.5.cloned.1.call-start = ((), (), s32[]{:S(2)}) async-start(), calls=%async_computation.1 | async-start | bytes 28901376 | tf_op jit(solution)/shard_map/all_gather | solution.py:152
  146.8 2.2 copy-start.14
  177.6 14.8 copy-start.24
  236.9 29.1 %copy-start.18 = (f32[8,8]{1,0:T(8,128)}, f32[8,8]{1,0:T(8,128)S(1)}, u32[]{:S(2)}) copy-start(f32[8,8]{1,0:T(8,128)S(1)} %fusion.1083) | copy-start | bytes 772
  296.7 16.4 copy-start.26
  386.5 11.9 copy-start.28
  403.4 32.4 %copy-start.6 = (f32[16,16]{1,0:T(8,128)}, f32[16,16]{1,0:T(8,128)S(1)}, u32[]{:S(2)}) copy-start(f32[16,16]{1,0:T(8,128)S(1)} %fusion.583) | copy-start | bytes 3076
  419.1 11.5 copy-start.30
  451.8 12.7 copy-start.32
  469.0 31.0 %copy-start.8 = (f32[16,16]{1,0:T(8,128)}, f32[16,16]{1,0:T(8,128)S(1)}, u32[]{:S(2)}) copy-start(f32[16,16]{1,0:T(8,128)S(1)} %fusion.579) | copy-start | bytes 3076
  484.7 11.7 copy-start.34
  518.4 12.7 copy-start.36
  535.3 32.8 %copy-start.10 = (f32[16,16]{1,0:T(8,128)}, f32[16,16]{1,0:T(8,128)S(1)}, u32[]{:S(2)}) copy-start(f32[16,16]{1,0:T(8,128)S(1)} %fusion.575) | copy-start | bytes 3076
  551.1 11.5 copy-start.38
  583.8 11.9 copy-start.40
  600.7 278.3 %copy-start.12 = (f32[16,16]{1,0:T(8,128)}, f32[16,16]{1,0:T(8,128)S(1)}, u32[]{:S(2)}) copy-start(f32[16,16]{1,0:T(8,128)S(1)} %fusion.571) | copy-start | bytes 3076
  616.1 262.9 %copy-start.42 = (f32[8,8]{1,0:T(8,128)}, f32[8,8]{1,0:T(8,128)S(1)}, u32[]{:S(2)}) copy-start(f32[8,8]{1,0:T(8,128)S(1)} %fusion.1043) | copy-start | bytes 772
  634.2 244.7 %copy-start = (f32[1024,128]{0,1:T(8,128)}, f32[1024,128]{0,1:T(8,128)S(1)}, u32[]{:S(2)}) copy-start(f32[1024,128]{0,1:T(8,128)S(1)} %fusion.181) | copy-start | bytes 1572868
  635.4 243.5 %copy-start.2 = (f32[1024,128]{1,0:T(8,128)}, f32[1024,128]{1,0:T(8,128)S(1)}, u32[]{:S(2)}) copy-start(f32[1024,128]{1,0:T(8,128)S(1)} %copy.1064) | copy-start | bytes 1572868
  655.5 320.8 %all-reduce.188.cloned.1.call-start = ((), (), s32[]{:S(2)}) async-start(), calls=%async_computation.3 | async-start | bytes 262144 | tf_op jit(solution)/shard_map/psum | solution.py:114
  891.7 29.9 %copy-start.60 = (pred[1024]{0:T(1024)(128)(4,1)S(1)}, pred[1024]{0:T(1024)(128)(4,1)}, u32[]{:S(2)}) copy-start(pred[1024]{0:T(1024)(128)(4,1)} %fusion.1094) | copy-start | bytes 3076
  891.7 31.5 %copy-start.61 = (pred[8,8]{0,1:T(8,128)(4,1)S(1)}, pred[8,8]{0,1:T(8,128)(4,1)}, u32[]{:S(2)}) copy-start(pred[8,8]{0,1:T(8,128)(4,1)} %iota_compare_fusion.79) | copy-start | bytes 196
  922.8 792.7 %all-gather.7.cloned.1.call-start = ((), (), s32[]{:S(2)}) async-start(), calls=%async_computation.2 | async-start | bytes 28311552 | tf_op jit(solution)/shard_map/all_gather | solution.py:152
  1312.0 185.2 %copy-start.29 = (f32[8,8]{1,0:T(8,128)S(1)}, f32[8,8]{1,0:T(8,128)}, u32[]{:S(2)}) copy-start(f32[8,8]{1,0:T(8,128)} %copy-done.28) | copy-start | bytes 772
  1312.1 185.3 %copy-start.31 = (f32[8,8]{1,0:T(8,128)S(1)}, f32[8,8]{1,0:T(8,128)}, u32[]{:S(2)}) copy-start(f32[8,8]{1,0:T(8,128)} %copy-done.30) | copy-start | bytes 772
  1312.1 185.3 %copy-start.7 = (f32[16,16]{1,0:T(8,128)S(1)}, f32[16,16]{1,0:T(8,128)}, u32[]{:S(2)}) copy-start(f32[16,16]{1,0:T(8,128)} %copy-done.6) | copy-start | bytes 3076
  1312.1 185.4 %copy-start.33 = (f32[8,8]{1,0:T(8,128)S(1)}, f32[8,8]{1,0:T(8,128)}, u32[]{:S(2)}) copy-start(f32[8,8]{1,0:T(8,128)} %copy-done.32) | copy-start | bytes 772
  1312.1 185.4 %copy-start.35 = (f32[8,8]{1,0:T(8,128)S(1)}, f32[8,8]{1,0:T(8,128)}, u32[]{:S(2)}) copy-start(f32[8,8]{1,0:T(8,128)} %copy-done.34) | copy-start | bytes 772
  1312.1 185.5 %copy-start.9 = (f32[16,16]{1,0:T(8,128)S(1)}, f32[16,16]{1,0:T(8,128)}, u32[]{:S(2)}) copy-start(f32[16,16]{1,0:T(8,128)} %copy-done.8) | copy-start | bytes 3076
  1312.7 185.0 %copy-start.37 = (f32[8,8]{1,0:T(8,128)S(1)}, f32[8,8]{1,0:T(8,128)}, u32[]{:S(2)}) copy-start(f32[8,8]{1,0:T(8,128)} %copy-done.36) | copy-start | bytes 772
  1312.7 185.1 %copy-start.39 = (f32[8,8]{1,0:T(8,128)S(1)}, f32[8,8]{1,0:T(8,128)}, u32[]{:S(2)}) copy-start(f32[8,8]{1,0:T(8,128)} %copy-done.38) | copy-start | bytes 772
  1312.8 185.2 %copy-start.11 = (f32[16,16]{1,0:T(8,128)S(1)}, f32[16,16]{1,0:T(8,128)}, u32[]{:S(2)}) copy-start(f32[16,16]{1,0:T(8,128)} %copy-done.10) | copy-start | bytes 3076
  1312.8 185.2 %copy-start.41 = (f32[8,8]{1,0:T(8,128)S(1)}, f32[8,8]{1,0:T(8,128)}, u32[]{:S(2)}) copy-start(f32[8,8]{1,0:T(8,128)} %copy-done.40) | copy-start | bytes 772
  1312.8 185.3 %copy-start.13 = (f32[16,16]{1,0:T(8,128)S(1)}, f32[16,16]{1,0:T(8,128)}, u32[]{:S(2)}) copy-start(f32[16,16]{1,0:T(8,128)} %copy-done.12) | copy-start | bytes 3076
  1312.8 185.3 %copy-start.43 = (f32[8,8]{1,0:T(8,128)S(1)}, f32[8,8]{1,0:T(8,128)}, u32[]{:S(2)}) copy-start(f32[8,8]{1,0:T(8,128)} %copy-done.42) | copy-start | bytes 772
  1312.8 185.6 %copy-start.15 = (f32[8,8]{1,0:T(8,128)S(1)}, f32[8,8]{1,0:T(8,128)}, u32[]{:S(2)}) copy-start(f32[8,8]{1,0:T(8,128)} %copy-done.14) | copy-start | bytes 772
  1312.8 185.6 %copy-start.17 = (f32[8,8]{1,0:T(8,128)S(1)}, f32[8,8]{1,0:T(8,128)}, u32[]{:S(2)}) copy-start(f32[8,8]{1,0:T(8,128)} %copy-done.16) | copy-start | bytes 772
  1312.8 185.7 %copy-start.21 = (f32[8,8]{1,0:T(8,128)S(1)}, f32[8,8]{1,0:T(8,128)}, u32[]{:S(2)}) copy-start(f32[8,8]{1,0:T(8,128)} %copy-done.20) | copy-start | bytes 772
  1312.8 185.8 %copy-start.23 = (f32[8,8]{1,0:T(8,128)S(1)}, f32[8,8]{1,0:T(8,128)}, u32[]{:S(2)}) copy-start(f32[8,8]{1,0:T(8,128)} %copy-done.22) | copy-start | bytes 772
  1312.8 185.8 %copy-start.46 = (f32[8,8]{0,1:T(8,128)S(1)}, f32[8,8]{0,1:T(8,128)}, u32[]{:S(2)}) copy-start(f32[8,8]{0,1:T(8,128)} %get-tuple-element.511) | copy-start | bytes 772
  1312.8 185.8 %copy-start.47 = (f32[8,8]{0,1:T(8,128)S(1)}, f32[8,8]{0,1:T(8,128)}, u32[]{:S(2)}) copy-start(f32[8,8]{0,1:T(8,128)} %get-tuple-element.509) | copy-start | bytes 772
  1313.0 185.8 %copy-start.48 = (f32[8,8]{0,1:T(8,128)S(1)}, f32[8,8]{0,1:T(8,128)}, u32[]{:S(2)}) copy-start(f32[8,8]{0,1:T(8,128)} %get-tuple-element.503) | copy-start | bytes 772
  1313.0 185.8 %copy-start.49 = (f32[8,8]{0,1:T(8,128)S(1)}, f32[8,8]{0,1:T(8,128)}, u32[]{:S(2)}) copy-start(f32[8,8]{0,1:T(8,128)} %get-tuple-element.501) | copy-start | bytes 772
  1313.1 185.7 %copy-start.52 = (f32[8,8]{0,1:T(8,128)S(1)}, f32[8,8]{0,1:T(8,128)}, u32[]{:S(2)}) copy-start(f32[8,8]{0,1:T(8,128)} %get-tuple-element.495) | copy-start | bytes 772
  1313.1 185.7 %copy-start.53 = (f32[8,8]{0,1:T(8,128)S(1)}, f32[8,8]{0,1:T(8,128)}, u32[]{:S(2)}) copy-start(f32[8,8]{0,1:T(8,128)} %get-tuple-element.493) | copy-start | bytes 772
  1313.4 185.5 %copy-start.54 = (f32[8,8]{0,1:T(8,128)S(1)}, f32[8,8]{0,1:T(8,128)}, u32[]{:S(2)}) copy-start(f32[8,8]{0,1:T(8,128)} %get-tuple-element.487) | copy-start | bytes 772
  1313.4 185.5 %copy-start.55 = (f32[8,8]{0,1:T(8,128)S(1)}, f32[8,8]{0,1:T(8,128)}, u32[]{:S(2)}) copy-start(f32[8,8]{0,1:T(8,128)} %get-tuple-element.485) | copy-start | bytes 772
  1313.6 185.4 %copy-start.25 = (f32[8,8]{1,0:T(8,128)S(1)}, f32[8,8]{1,0:T(8,128)}, u32[]{:S(2)}) copy-start(f32[8,8]{1,0:T(8,128)} %copy-done.24) | copy-start | bytes 772
  1313.9 185.2 %copy-start.27 = (f32[8,8]{1,0:T(8,128)S(1)}, f32[8,8]{1,0:T(8,128)}, u32[]{:S(2)}) copy-start(f32[8,8]{1,0:T(8,128)} %copy-done.26) | copy-start | bytes 772
  1314.1 185.1 %copy-start.56 = (f32[8,8]{0,1:T(8,128)S(1)}, f32[8,8]{0,1:T(8,128)}, u32[]{:S(2)}) copy-start(f32[8,8]{0,1:T(8,128)} %get-tuple-element.507) | copy-start | bytes 772
  1314.1 185.1 %copy-start.57 = (f32[8,8]{0,1:T(8,128)S(1)}, f32[8,8]{0,1:T(8,128)}, u32[]{:S(2)}) copy-start(f32[8,8]{0,1:T(8,128)} %get-tuple-element.505) | copy-start | bytes 772
  1314.6 184.6 %copy-start.58 = (f32[8,8]{0,1:T(8,128)S(1)}, f32[8,8]{0,1:T(8,128)}, u32[]{:S(2)}) copy-start(f32[8,8]{0,1:T(8,128)} %get-tuple-element.491) | copy-start | bytes 772
  1314.6 184.6 %copy-start.59 = (f32[8,8]{0,1:T(8,128)S(1)}, f32[8,8]{0,1:T(8,128)}, u32[]{:S(2)}) copy-start(f32[8,8]{0,1:T(8,128)} %get-tuple-element.489) | copy-start | bytes 772
  1314.8 184.6 %copy-start.19 = (f32[8,8]{1,0:T(8,128)S(1)}, f32[8,8]{1,0:T(8,128)}, u32[]{:S(2)}) copy-start(f32[8,8]{1,0:T(8,128)} %copy-done.18) | copy-start | bytes 772
  1315.4 184.0 %copy-start.50 = (f32[8,8]{0,1:T(8,128)S(1)}, f32[8,8]{0,1:T(8,128)}, u32[]{:S(2)}) copy-start(f32[8,8]{0,1:T(8,128)} %get-tuple-element.499) | copy-start | bytes 772
  1315.4 184.0 %copy-start.51 = (f32[8,8]{0,1:T(8,128)S(1)}, f32[8,8]{0,1:T(8,128)}, u32[]{:S(2)}) copy-start(f32[8,8]{0,1:T(8,128)} %get-tuple-element.497) | copy-start | bytes 772
  1316.2 183.4 %copy-start.4 = (f32[1024,128]{0,1:T(8,128)S(1)}, f32[1024,128]{0,1:T(8,128)}, u32[]{:S(2)}) copy-start(f32[1024,128]{0,1:T(8,128)} %get-tuple-element.512) | copy-start | bytes 1572868
  1316.2 183.4 %copy-start.44 = (f32[8,8]{0,1:T(8,128)S(1)}, f32[8,8]{0,1:T(8,128)}, u32[]{:S(2)}) copy-start(f32[8,8]{0,1:T(8,128)} %get-tuple-element.483) | copy-start | bytes 772
  1316.2 183.3 %copy-start.45 = (f32[8,8]{0,1:T(8,128)S(1)}, f32[8,8]{0,1:T(8,128)}, u32[]{:S(2)}) copy-start(f32[8,8]{0,1:T(8,128)} %get-tuple-element.481) | copy-start | bytes 772
  1477.3 238.2 %copy-start.1 = (f32[1024,128]{1,0:T(8,128)}, f32[1024,128]{1,0:T(8,128)S(1)}, u32[]{:S(2)}) copy-start(f32[1024,128]{1,0:T(8,128)S(1)} %constant_dynamic-update-slice_fusion) | copy-start | bytes 1572868
  1728.0 26.3 %copy-start.5 = (f32[1024,128]{1,0:T(8,128)S(1)}, f32[1024,128]{1,0:T(8,128)}, u32[]{:S(2)}) copy-start(f32[1024,128]{1,0:T(8,128)} %copy.2121) | copy-start | bytes 1572868
  (3 other events, 4.5 us)
Sparse Core Ops, SparseCore 0:
  11.6 55.1 all-reduce.185
  70.9 55.1 all-reduce.189
  655.6 223.2 all-gather.4
  923.0 53.2 all-reduce.187
  1496.5 218.9 all-gather.6
